TPU v7x, 256 devices: a whole 4x4x8 slice. The times are simulated.
256 devices in a mesh: seq: 32 (over y, z), tp: 8 (over x, core).
Axes of the slice: x: 4, y: 4, z: 8, core: 2. Of those that a mesh axis runs over, the one named last changes fastest.
Arguments:
- tokens: bfloat16 [24576, 2048], P('seq', 'tp'), may hold values from -20 to 20
- w_query: bfloat16 [2048, 2048], P(None, 'tp'), may hold values from -0.125 to 0.125
- w_key: bfloat16 [2048, 2048], P(None, 'tp'), may hold values from -0.125 to 0.125
- w_value: bfloat16 [2048, 2048], P(None, 'tp'), may hold values from -0.125 to 0.125
- head_gain: float32 [2048], P('tp'), may hold values from 0.5 to 1.5
- w_out: bfloat16 [2048, 2048], P('tp'), may hold values from -0.125 to 0.125
- norm_gain: float32 [2048], replicated, may hold values from 0.5 to 1.5
- w_gate: bfloat16 [2048, 8192], P('seq', 'tp'), may hold values from -0.125 to 0.125
- w_up: bfloat16 [2048, 8192], P('seq', 'tp'), may hold values from -0.125 to 0.125
- w_down: bfloat16 [8192, 2048], P('tp', 'seq'), may hold values from -0.0625 to 0.0625
Outputs:
- layer_out: bfloat16 [24576, 2048], P('seq', 'tp')
All inputs are finite; a program needn't handle non-finite values.
Results may differ from a plain program's by a relative error of at most 0.009.
Values may be sent and summed in bfloat16 or wider, within the bound.
No kernel may reach another device: no remote copies, remote signals or barrier semaphores. Data moves between devices by JAX's collectives and lax.ppermute only.
A program may use at most 128 MiB of HBM per device.

v0:
```python
import jax
import jax.numpy as jnp
from jax import lax
from jax.sharding import Mesh
from jax.sharding import PartitionSpec as P

HD = 128
SEQ = ("seq_0", "seq_1")


def nothing_yet(array, identity):
    return jnp.zeros_like(array) + jnp.asarray(identity, array.dtype)


def entering(array, axes, combine, identity):
    before = start = nothing_yet(array, identity)
    total = array
    for axis in reversed(axes):
        peers, position = (lax.axis_size(axis), lax.axis_index(axis))
        pieces = lax.all_gather(total.astype(jnp.bfloat16), axis)
        inside, total = (start, start)
        for k in range(peers):
            passed = k < position
            total = combine(total, pieces[k].astype(array.dtype))
            inside = jnp.where(passed, total, inside)
        before = combine(inside, before)
    return before


def in_one_piece(arrays, axis, dim, along):
    ends, at = ([], 0)
    for a in arrays[:-1]:
        at += a.shape[along]
        ends.append(at)
    both = jnp.concatenate(arrays, axis=along)
    return tuple(jnp.split(lax.all_gather(both, axis, axis=dim, tiled=True), ends, axis=along))


def split_up(array, dim, peers):
    shape = array.shape
    tiles = array.reshape(*shape[:dim], peers, shape[dim] // peers, *shape[dim + 1 :])
    return jnp.moveaxis(tiles, dim, 0)


def sum_at_owner(array, axis, dim):
    tiles = split_up(array, dim, lax.axis_size(axis))
    arrived = lax.all_to_all(tiles, axis, split_axis=0, concat_axis=0, tiled=True)
    return arrived.astype(jnp.float32).sum(axis=0)


def add_states(earlier, later):
    return earlier + later


def body(tokens, w_query, w_key, w_value, head_gain, w_out, norm_gain, w_gate, w_up, w_down):
    length = tokens.shape[0]
    width_here = tokens.shape[1]
    heads_here = w_query.shape[1] // HD
    features = lax.all_gather(tokens, "tp", axis=1, tiled=True)

    def project(weight):
        product = jnp.dot(features, weight, preferred_element_type=jnp.float32)
        return product.astype(jnp.bfloat16).reshape(length, heads_here, HD)

    query = project(w_query)
    keys_local = project(w_key)
    values_local = project(w_value)
    scores = jnp.einsum("ihd,jhd->hij", query, keys_local, preferred_element_type=jnp.float32)
    causal = jnp.arange(length)[:, None] >= jnp.arange(length)[None, :]
    scores = jnp.where(causal[None], scores, 0.0).astype(jnp.bfloat16)
    inside = jnp.einsum("hij,jhd->ihd", scores, values_local, preferred_element_type=jnp.float32)
    own_state = jnp.einsum(
        "jhd,jhe->hde", keys_local, values_local, preferred_element_type=jnp.float32
    )
    history = entering(own_state, SEQ, add_states, jnp.zeros_like(own_state))
    carried = jnp.einsum(
        "ihd,hde->ihe", query, history.astype(jnp.bfloat16), preferred_element_type=jnp.float32
    )
    mixed = inside + carried
    scale = lax.rsqrt(jnp.mean(mixed * mixed, axis=-1, keepdims=True) + 1e-06)
    normed = (mixed * scale * head_gain.reshape(heads_here, HD)).astype(jnp.bfloat16)
    normed = normed.reshape(length, heads_here * HD)
    partial_value = jnp.dot(normed, w_out, preferred_element_type=jnp.float32)
    own_column = lax.axis_index("tp") * width_here
    summed = lax.psum(partial_value.astype(jnp.bfloat16), "tp").astype(jnp.float32)
    resid_whole = features.astype(jnp.float32) + summed
    factor = lax.rsqrt(jnp.mean(resid_whole * resid_whole, axis=-1, keepdims=True) + 1e-05)
    ffn_in = (resid_whole * factor * norm_gain).astype(jnp.bfloat16)
    resid = lax.dynamic_slice_in_dim(resid_whole, own_column, width_here, 1)
    pieces = in_one_piece((w_gate, w_up), SEQ, 0, 1)
    gate_sum = jnp.dot(ffn_in, pieces[0], preferred_element_type=jnp.float32)
    upward_sum = jnp.dot(ffn_in, pieces[1], preferred_element_type=jnp.float32)
    hidden = (jax.nn.silu(gate_sum) * upward_sum).astype(jnp.bfloat16)
    terms = jnp.dot(
        hidden, lax.all_gather(w_down, SEQ, axis=1, tiled=True), preferred_element_type=jnp.float32
    )
    mlp_share = sum_at_owner(terms.astype(jnp.bfloat16), "tp", 1)
    return (resid + mlp_share).astype(jnp.bfloat16)


def solution(mesh):
    finer = Mesh(mesh.devices.reshape(4, 8, mesh.shape["tp"]), ("seq_0", "seq_1", "tp"))
    return jax.shard_map(
        body,
        mesh=finer,
        in_specs=(
            P(SEQ, "tp"),
            P(None, "tp"),
            P(None, "tp"),
            P(None, "tp"),
            P("tp"),
            P("tp", None),
            P(),
            P(SEQ, "tp"),
            P(SEQ, "tp"),
            P("tp", SEQ),
        ),
        out_specs=P(SEQ, "tp"),
        check_vma=False,
    )
```

profile of v0, /device:TPU:1, one launch (start us, length us, event | category | flops | bytes accessed | tf_op | source)
XLA Modules:
  0.0 356.1 jit_solution(3774338087254047791)
XLA Ops:
  7.4 0.0 copy-start
  7.4 0.0 all-gather.5.cloned.1.call-start
  7.4 0.7 all-gather.5.cloned.1.call-update
  8.1 0.0 all-reduce.2.cloned.1.call-start
  8.2 0.2 iota_compare_fusion
  8.3 39.5 %all-gather.5.cloned.1.call-done = bf16[768,2048]{1,0:T(8,128)(2,1)} async-done(((bf16[768,256]{1,0:T(8,128)(2,1)}), bf16[768,2048]{1,0:T(8,128)(2,1)}) %all-gather.5.cloned.1.call-update) | async-done | bytes 3145744 | tf_op jit(solution)/shard_map/all_gather | solution.py:59
  47.9 0.0 copy-start.1
  47.9 3.3 convolution_convert_fusion.2
  51.2 0.0 copy-done.1
  51.2 0.0 copy-start.5
  51.2 2.4 convolution_convert_fusion.4
  53.6 0.3 convolution_convert_fusion.5
  53.9 20.8 %all-gather = bf16[16,128,128]{2,1,0:T(8,128)(2,1)S(1)} all-gather(bf16[2,128,128]{2,1,0:T(8,128)(2,1)S(1)} %convolution_convert_fusion.5), channel_id=2, replica_groups=mesh['seq_0'=4,'seq_1'=8,'tp'=8] {'seq_1'}, dimensions={0}, use_global_device_ids=true | all-gather | bytes 589824 | tf_op jit(solution)/shard_map/all_gather | solution.py:20
  74.7 0.1 fusion.28
  74.7 9.7 %all_gather.22 = bf16[4,2,128,128]{3,2,1,0:T(8,128)(2,1)S(1)} all-gather(bf16[1,2,128,128]{3,2,1,0:T(8,128)(2,1)S(1)} %fusion.28), channel_id=1, replica_groups=mesh['seq_0'=4,'seq_1'=8,'tp'=8] {'seq_0'}, dimensions={0}, use_global_device_ids=true | all-gather | bytes 327680 | tf_op jit(solution)/shard_map/all_gather | solution.py:20
  84.5 0.0 copy-done.5
  84.5 1.1 convolution_convert_fusion.3
  85.6 0.0 copy-start.7
  85.6 0.7 copy-done.7
  86.3 1.3 fusion.29
  87.6 0.0 copy-start.4
  87.6 2.9 multiply_reduce_fusion.1
  90.5 0.0 copy-done.4
  90.5 0.1 multiply_convert_fusion.2
  90.6 0.0 copy-done
  90.6 2.7 convolution_convert_fusion.1
  93.4 0.0 copy-start.2
  93.4 0.0 copy-start.3
  93.4 0.0 all-reduce.2.cloned.1.call-update
  93.4 0.0 all-gather.7.cloned.1.call-start
  93.5 0.8 copy-done.2
  94.3 0.1 copy-done.3
  94.3 0.7 pad_maximum_fusion
  95.1 0.0 all-gather.7.cloned.1.call-update
  95.1 0.2 all-gather.9.cloned.1.call-start
  95.3 0.4 all-gather.9.cloned.1.call-update
  95.7 0.0 copy-start.6
  95.7 79.1 %all-reduce.2.cloned.1.call-done = bf16[768,2048]{1,0:T(8,128)(2,1)} async-done(((bf16[768,2048]{1,0:T(8,128)(2,1)}), bf16[768,2048]{1,0:T(8,128)(2,1)}) %all-reduce.2.cloned.1.call-update) | async-done | bytes 3145744 | tf_op jit(solution)/shard_map/psum | solution.py:85
  174.8 6.7 %convert_add_fusion = (f32[768,2048]{1,0:T(8,128)}, f32[768]{0:T(1024)S(1)}) fusion(bf16[768,2048]{1,0:T(8,128)(2,1)} %all-reduce.2.cloned.1.call-done, bf16[768,2048]{1,0:T(8,128)(2,1)} %all-gather.5.cloned.1.call-done), kind=kLoop, calls=%fused_computation.3 | loop fusion | flops 7863552 | bytes 12585984 | tf_op jit(solution)/shard_map/add | solution.py:86
  181.6 19.3 %all-gather.7.cloned.1.call-done = bf16[2048,2048]{1,0:T(8,128)(2,1)} async-done(((bf16[64,2048]{1,0:T(8,128)(2,1)}), bf16[2048,2048]{1,0:T(8,128)(2,1)}) %all-gather.7.cloned.1.call-update) | async-done | bytes 8388624 | tf_op jit(solution)/shard_map/all_gather | solution.py:36
  200.9 0.0 copy-done.6
  200.9 9.2 %fusion = f32[768,1024]{1,0:T(8,128)} fusion(bf16[2048,2048]{1,0:T(8,128)(2,1)} %all-gather.7.cloned.1.call-done, f32[2048]{0:T(1024)S(1)} %copy-done.6, f32[768]{0:T(1024)S(1)} %add_rsqrt_fusion.1, bf16[768,2048]{1,0:T(8,128)(2,1)} %all-reduce.2.cloned.1.call-done, bf16[768,2048]{1,0:T(8,128)(2,1)} %all-gather.5.cloned.1.call-done), kind=kOutput, calls=%fused_computation.5 | convolution fusion | flops 3230662656 | bytes 13642752 | tf_op jit(solution)/shard_map/dot_general | solution.py:92
  210.2 69.3 %all-gather.9.cloned.1.call-done = bf16[1024,2048]{0,1:T(8,128)(2,1)} async-done(((bf16[1024,64]{0,1:T(8,128)(2,1)}), bf16[1024,2048]{0,1:T(8,128)(2,1)}) %all-gather.9.cloned.1.call-update) | async-done | bytes 4194320 | tf_op jit(solution)/shard_map/all_gather | solution.py:95
  279.5 14.9 %convolution_convert_fusion = bf16[768,2048]{1,0:T(8,128)(2,1)} fusion(bf16[1024,2048]{0,1:T(8,128)(2,1)} %all-gather.9.cloned.1.call-done, f32[768,1024]{1,0:T(8,128)} %fusion, bf16[2048,2048]{1,0:T(8,128)(2,1)} %all-gather.7.cloned.1.call-done, f32[2048]{0:T(1024)S(1)} %copy-done.6, f32[768]{0:T(1024)S(1)} %add_rsqrt_fusion.1, ...), kind=kOutput, calls=%fused_computation.9 | convolution fusion | flops 6458179584 | bytes 20982784 | tf_op jit(solution)/shard_map/dot_general | solution.py:94
  294.4 3.7 %copy.23 = bf16[96,8,8,256]{3,2,0,1:T(8,128)(2,1)} copy(bf16[96,8,8,256]{3,2,1,0:T(8,128)(2,1)} %bitcast.58) | data formatting | bytes 6291456 | tf_op jit(solution)/shard_map/reshape | solution.py:41
  298.1 8.6 %all-to-all-start = ((bf16[8,768,256]{2,1,0:T(8,128)(2,1)}), bf16[8,768,256]{2,1,0:T(8,128)(2,1)}, u32[]{:S(2)}, u32[]{:S(2)}) async-start(bf16[8,768,256]{2,1,0:T(8,128)(2,1)} %bitcast.57), calls=%async_computation | async-start | bytes 6291456 | tf_op jit(solution)/shard_map/all_to_all | solution.py:47
  306.7 37.6 %all-to-all-done = bf16[8,768,256]{2,1,0:T(8,128)(2,1)} async-done(((bf16[8,768,256]{2,1,0:T(8,128)(2,1)}), bf16[8,768,256]{2,1,0:T(8,128)(2,1)}, u32[]{:S(2)}, u32[]{:S(2)}) %all-to-all-start) | async-done | bytes 3145760 | tf_op jit(solution)/shard_map/all_to_all | solution.py:47
  344.3 2.4 convert_reduce_fusion
  346.7 2.0 add_convert_fusion
  (2 shorter events, 0.0 us)
Async XLA Ops:
  7.4 83.3 %copy-start = (bf16[256,2048]{1,0:T(8,128)(2,1)S(1)}, bf16[256,2048]{1,0:T(8,128)(2,1)}, u32[]{:S(2)}) copy-start(bf16[256,2048]{1,0:T(8,128)(2,1)} %param.15) | copy-start | bytes 3145732
  7.4 40.5 %all-gather.5.cloned.1.call-start = ((), (), s32[]{:S(2)}) async-start(), calls=%async_computation.1 | async-start | bytes 3538944 | tf_op jit(solution)/shard_map/all_gather | solution.py:59
  8.1 166.7 %all-reduce.2.cloned.1.call-start = ((), (), s32[]{:S(2)}) async-start(), calls=%async_computation.2 | async-start | bytes 6291456 | tf_op jit(solution)/shard_map/psum | solution.py:85
  47.9 3.4 copy-start.1
  51.2 33.2 %copy-start.5 = (bf16[2048,256]{1,0:T(8,128)(2,1)S(1)}, bf16[2048,256]{1,0:T(8,128)(2,1)}, u32[]{:S(2)}) copy-start(bf16[2048,256]{1,0:T(8,128)(2,1)} %param.11) | copy-start | bytes 3145732
  85.6 0.7 copy-start.7
  87.6 2.9 copy-start.4
  93.4 0.9 copy-start.2
  93.4 1.0 copy-start.3
  93.4 107.5 %all-gather.7.cloned.1.call-start = ((), (), s32[]{:S(2)}) async-start(), calls=%async_computation.3 | async-start | bytes 8650752 | tf_op jit(solution)/shard_map/all_gather | solution.py:36
  95.1 184.4 %all-gather.9.cloned.1.call-start = ((), (), s32[]{:S(2)}) async-start(), calls=%async_computation.4 | async-start | bytes 4325376 | tf_op jit(solution)/shard_map/all_gather | solution.py:95
  95.7 105.2 %copy-start.6 = (f32[2048]{0:T(1024)S(1)}, f32[2048]{0:T(1024)}, u32[]{:S(2)}) copy-start(f32[2048]{0:T(1024)} %param.16) | copy-start | bytes 24580
  298.1 46.2 %all-to-all-start = ((bf16[8,768,256]{2,1,0:T(8,128)(2,1)}), bf16[8,768,256]{2,1,0:T(8,128)(2,1)}, u32[]{:S(2)}, u32[]{:S(2)}) async-start(bf16[8,768,256]{2,1,0:T(8,128)(2,1)} %bitcast.57), calls=%async_computation | async-start | bytes 6291456 | tf_op jit(solution)/shard_map/all_to_all | solution.py:47
Sparse Core Ops, SparseCore 0:
  10.0 37.8 all-gather.4
  93.5 81.2 all-reduce.1
Sparse Core Ops, SparseCore 1:
  96.5 104.4 all-gather.6
  203.4 76.1 all-gather.8
where the time goes:
time: 356 us
  waiting for transfers between devices  246 us (69%)
  matrix products  38.1 us (11%)
  blocking collectives  30.5 us (9%)
  between operations  15 us (4%)
  other arithmetic  12.2 us (3%)
  starting transfers between devices  8.92 us (3%)
  local copies, waits for them, and re-layouts  5.37 us (2%)
    psum x1, waiting for transfers between devices, body(): lax.psum(partial_value.astype(jnp.bfloat16), 'tp').astype(jnp.float32)  79.1 us
    all_gather x1, waiting for transfers between devices, body(): lax.all_gather(w_down, SEQ, axis=1, tiled=True)  69.3 us
    all_gather x1, waiting for transfers between devices, body(): features = lax.all_gather(tokens, 'tp', axis=1, tiled=True)  39.5 us
    all_to_all x1, waiting for transfers between devices, sum_at_owner(): lax.all_to_all(tiles, axis, split_axis=0, concat_axis=0, tiled=True)  37.6 us
    all_gather x2, blocking collectives, entering(): pieces = lax.all_gather(total.astype(jnp.bfloat16), axis)  30.5 us
    all_gather x1, waiting for transfers between devices, in_one_piece(): lax.all_gather(both, axis, axis=dim, tiled=True)  19.3 us
    dot_general x1, matrix products, body(): jnp.dot(hidden, lax.all_gather(w_down, SEQ, axis=1, tiled=True), preferre...  14.9 us
    dot_general x1, matrix products, body(): upward_sum = jnp.dot(ffn_in, pieces[1], preferred_element_type=jnp.float32)  9.24 us
  transfers between devices with their start and end apart: 5, of which 5 were waited for; matrix products, arithmetic and copies ran while one was open for 5% of the time, Pallas kernels for 0%

commit v1 on v0

--- a/solution.py
+++ b/solution.py
@@ -56,7 +56,7 @@
     length = tokens.shape[0]
     width_here = tokens.shape[1]
     heads_here = w_query.shape[1] // HD
-    features = lax.all_gather(tokens, "tp", axis=1, tiled=True)
+    features = jnp.concatenate(lax.all_gather(tokens, "tp"), axis=1)
 
     def project(weight):
         product = jnp.dot(features, weight, preferred_element_type=jnp.float32)

time: 356 us -> 351 us (0.986)
  waiting for transfers between devices: 246 us -> 242 us
  matrix products: 38.1 us -> 34.4 us
    dot_general x3, matrix products: 6.82 us -> 3.09 us  [project(): product = jnp.dot(features, weight, preferred_element_type=jnp.float32)]
where the time goes in v1:
time: 351 us
  waiting for transfers between devices  242 us (69%)
  matrix products  34.4 us (10%)
  blocking collectives  30.5 us (9%)
  between operations  15 us (4%)
  other arithmetic  12.3 us (4%)
  starting transfers between devices  8.94 us (3%)
  local copies, waits for them, and re-layouts  8.15 us (2%)
    psum x1, waiting for transfers between devices, body(): lax.psum(partial_value.astype(jnp.bfloat16), 'tp').astype(jnp.float32)  77.9 us
    all_gather x1, waiting for transfers between devices, body(): lax.all_gather(w_down, SEQ, axis=1, tiled=True)  69.3 us
    all_to_all x1, waiting for transfers between devices, sum_at_owner(): lax.all_to_all(tiles, axis, split_axis=0, concat_axis=0, tiled=True)  37.6 us
    all_gather x1, waiting for transfers between devices, body(): features = jnp.concatenate(lax.all_gather(tokens, 'tp'), axis=1)  36.1 us
    all_gather x2, blocking collectives, entering(): pieces = lax.all_gather(total.astype(jnp.bfloat16), axis)  30.5 us
    all_gather x1, waiting for transfers between devices, in_one_piece(): lax.all_gather(both, axis, axis=dim, tiled=True)  19.6 us
    dot_general x1, matrix products, body(): jnp.dot(hidden, lax.all_gather(w_down, SEQ, axis=1, tiled=True), preferre...  14.9 us
    dot_general x1, matrix products, body(): upward_sum = jnp.dot(ffn_in, pieces[1], preferred_element_type=jnp.float32)  9.25 us
  transfers between devices with their start and end apart: 5, of which 5 were waited for; matrix products, arithmetic and copies ran while one was open for 5% of the time, Pallas kernels for 0%

profile of v1, /device:TPU:1, one launch (start us, length us, event | category | flops | bytes accessed | tf_op | source)
XLA Modules:
  0.0 350.8 jit_solution(10659116007552938657)
XLA Ops:
  7.4 0.0 copy-start
  7.4 0.0 all-gather.10.cloned.1.call-start
  7.4 0.7 all-gather.10.cloned.1.call-update
  8.1 0.0 all-reduce.2.cloned.1.call-start
  8.2 0.2 iota_compare_fusion
  8.3 36.1 %all-gather.10.cloned.1.call-done = bf16[6144,256]{1,0:T(8,128)(2,1)} async-done(((bf16[768,256]{1,0:T(8,128)(2,1)}), bf16[6144,256]{1,0:T(8,128)(2,1)}) %all-gather.10.cloned.1.call-update) | async-done | bytes 3145744 | tf_op jit(solution)/shard_map/all_gather | solution.py:59
  44.4 0.0 copy-start.5
  44.4 2.4 copy.24
  46.8 0.0 copy-start.1
  46.8 0.0 copy-start.6
  46.9 0.0 copy-done.5
  46.9 1.0 convolution_convert_fusion.2
  47.9 0.9 copy-done.6
  48.8 0.0 copy-start.7
  48.8 1.0 convolution_convert_fusion.3
  49.9 0.0 copy-done.1
  49.9 0.2 copy-done.7
  50.1 0.0 copy-start.9
  50.1 1.0 convolution_convert_fusion.4
  51.1 0.3 convolution_convert_fusion.5
  51.4 20.8 %all-gather.1 = bf16[16,128,128]{2,1,0:T(8,128)(2,1)S(1)} all-gather(bf16[2,128,128]{2,1,0:T(8,128)(2,1)S(1)} %convolution_convert_fusion.5), channel_id=3, replica_groups=mesh['seq_0'=4,'seq_1'=8,'tp'=8] {'seq_1'}, dimensions={0}, use_global_device_ids=true | all-gather | bytes 589824 | tf_op jit(solution)/shard_map/all_gather | solution.py:20
  72.1 0.1 fusion.28
  72.2 9.7 %all_gather.26 = bf16[4,2,128,128]{3,2,1,0:T(8,128)(2,1)S(1)} all-gather(bf16[1,2,128,128]{3,2,1,0:T(8,128)(2,1)S(1)} %fusion.28), channel_id=1, replica_groups=mesh['seq_0'=4,'seq_1'=8,'tp'=8] {'seq_0'}, dimensions={0}, use_global_device_ids=true | all-gather | bytes 327680 | tf_op jit(solution)/shard_map/all_gather | solution.py:20
  81.9 0.0 copy-done.9
  81.9 1.3 fusion.29
  83.2 0.0 copy-start.4
  83.2 2.9 multiply_reduce_fusion.1
  86.2 0.0 copy-done.4
  86.2 0.1 multiply_convert_fusion.2
  86.3 0.0 copy-done
  86.3 2.8 convolution_convert_fusion.1
  89.0 0.0 copy-start.2
  89.0 0.0 copy-start.3
  89.0 0.0 all-reduce.2.cloned.1.call-update
  89.1 0.0 all-gather.6.cloned.1.call-start
  89.1 0.8 copy-done.2
  89.9 0.1 copy-done.3
  90.0 0.7 pad_maximum_fusion
  90.7 0.0 all-gather.6.cloned.1.call-update
  90.8 0.2 all-gather.8.cloned.1.call-start
  91.0 0.4 all-gather.8.cloned.1.call-update
  91.3 0.0 copy-start.8
  91.4 77.9 %all-reduce.2.cloned.1.call-done = bf16[768,2048]{1,0:T(8,128)(2,1)} async-done(((bf16[768,2048]{1,0:T(8,128)(2,1)}), bf16[768,2048]{1,0:T(8,128)(2,1)}) %all-reduce.2.cloned.1.call-update) | async-done | bytes 3145744 | tf_op jit(solution)/shard_map/psum | solution.py:85
  169.2 6.8 %convert_add_fusion = (f32[768,2048]{1,0:T(8,128)}, f32[768]{0:T(1024)S(1)}) fusion(bf16[768,2048]{1,0:T(8,128)(2,1)} %all-reduce.2.cloned.1.call-done, bf16[768,2048]{1,0:T(8,128)(2,1)} %bitcast.67), kind=kLoop, calls=%fused_computation.3 | loop fusion | flops 7863552 | bytes 12585984 | tf_op jit(solution)/shard_map/add | solution.py:86
  176.0 19.6 %all-gather.6.cloned.1.call-done = bf16[2048,2048]{1,0:T(8,128)(2,1)} async-done(((bf16[64,2048]{1,0:T(8,128)(2,1)}), bf16[2048,2048]{1,0:T(8,128)(2,1)}) %all-gather.6.cloned.1.call-update) | async-done | bytes 8388624 | tf_op jit(solution)/shard_map/all_gather | solution.py:36
  195.6 0.0 copy-done.8
  195.6 9.3 %fusion = f32[768,1024]{1,0:T(8,128)} fusion(bf16[2048,2048]{1,0:T(8,128)(2,1)} %all-gather.6.cloned.1.call-done, f32[2048]{0:T(1024)S(1)} %copy-done.8, f32[768]{0:T(1024)S(1)} %add_rsqrt_fusion.1, bf16[768,2048]{1,0:T(8,128)(2,1)} %all-reduce.2.cloned.1.call-done, bf16[768,2048]{1,0:T(8,128)(2,1)} %bitcast.68), kind=kOutput, calls=%fused_computation.5 | convolution fusion | flops 3230662656 | bytes 13642752 | tf_op jit(solution)/shard_map/dot_general | solution.py:92
  204.8 69.3 %all-gather.8.cloned.1.call-done = bf16[1024,2048]{0,1:T(8,128)(2,1)} async-done(((bf16[1024,64]{0,1:T(8,128)(2,1)}), bf16[1024,2048]{0,1:T(8,128)(2,1)}) %all-gather.8.cloned.1.call-update) | async-done | bytes 4194320 | tf_op jit(solution)/shard_map/all_gather | solution.py:95
  274.2 14.9 %convolution_convert_fusion = bf16[768,2048]{1,0:T(8,128)(2,1)} fusion(bf16[1024,2048]{0,1:T(8,128)(2,1)} %all-gather.8.cloned.1.call-done, f32[768,1024]{1,0:T(8,128)} %fusion, bf16[2048,2048]{1,0:T(8,128)(2,1)} %all-gather.6.cloned.1.call-done, f32[2048]{0:T(1024)S(1)} %copy-done.8, f32[768]{0:T(1024)S(1)} %add_rsqrt_fusion.1, ...), kind=kOutput, calls=%fused_computation.9 | convolution fusion | flops 6458179584 | bytes 20982784 | tf_op jit(solution)/shard_map/dot_general | solution.py:94
  289.0 3.7 %copy.27 = bf16[96,8,8,256]{3,2,0,1:T(8,128)(2,1)} copy(bf16[96,8,8,256]{3,2,1,0:T(8,128)(2,1)} %bitcast.71) | data formatting | bytes 6291456 | tf_op jit(solution)/shard_map/reshape | solution.py:41
  292.7 8.6 %all-to-all-start = ((bf16[8,768,256]{2,1,0:T(8,128)(2,1)}), bf16[8,768,256]{2,1,0:T(8,128)(2,1)}, u32[]{:S(2)}, u32[]{:S(2)}) async-start(bf16[8,768,256]{2,1,0:T(8,128)(2,1)} %bitcast.63), calls=%async_computation | async-start | bytes 6291456 | tf_op jit(solution)/shard_map/all_to_all | solution.py:47
  301.4 37.6 %all-to-all-done = bf16[8,768,256]{2,1,0:T(8,128)(2,1)} async-done(((bf16[8,768,256]{2,1,0:T(8,128)(2,1)}), bf16[8,768,256]{2,1,0:T(8,128)(2,1)}, u32[]{:S(2)}, u32[]{:S(2)}) %all-to-all-start) | async-done | bytes 3145760 | tf_op jit(solution)/shard_map/all_to_all | solution.py:47
  338.9 2.4 convert_reduce_fusion
  341.3 2.0 add_convert_fusion
  (2 shorter events, 0.0 us)
Async XLA Ops:
  7.4 78.9 %copy-start = (bf16[256,2048]{1,0:T(8,128)(2,1)S(1)}, bf16[256,2048]{1,0:T(8,128)(2,1)}, u32[]{:S(2)}) copy-start(bf16[256,2048]{1,0:T(8,128)(2,1)} %param.15) | copy-start | bytes 3145732
  7.4 37.1 %all-gather.10.cloned.1.call-start = ((), (), s32[]{:S(2)}) async-start(), calls=%async_computation.4 | async-start | bytes 3538944 | tf_op jit(solution)/shard_map/all_gather | solution.py:59
  8.1 161.1 %all-reduce.2.cloned.1.call-start = ((), (), s32[]{:S(2)}) async-start(), calls=%async_computation.1 | async-start | bytes 6291456 | tf_op jit(solution)/shard_map/psum | solution.py:85
  44.4 2.4 copy-start.5
  46.8 3.0 copy-start.1
  46.8 2.0 copy-start.6
  48.8 1.2 copy-start.7
  50.1 31.9 %copy-start.9 = (bf16[768,256]{0,1:T(8,128)(2,1)}, bf16[768,256]{0,1:T(8,128)(2,1)S(1)}, u32[]{:S(2)}) copy-start(bf16[768,256]{0,1:T(8,128)(2,1)S(1)} %convolution_convert_fusion.3) | copy-start | bytes 1179652
  83.2 2.9 copy-start.4
  89.0 0.9 copy-start.2
  89.0 1.0 copy-start.3
  89.1 106.5 %all-gather.6.cloned.1.call-start = ((), (), s32[]{:S(2)}) async-start(), calls=%async_computation.2 | async-start | bytes 8650752 | tf_op jit(solution)/shard_map/all_gather | solution.py:36
  90.8 183.4 %all-gather.8.cloned.1.call-start = ((), (), s32[]{:S(2)}) async-start(), calls=%async_computation.3 | async-start | bytes 4325376 | tf_op jit(solution)/shard_map/all_gather | solution.py:95
  91.3 104.2 %copy-start.8 = (f32[2048]{0:T(1024)S(1)}, f32[2048]{0:T(1024)}, u32[]{:S(2)}) copy-start(f32[2048]{0:T(1024)} %param.16) | copy-start | bytes 24580
  292.7 46.2 %all-to-all-start = ((bf16[8,768,256]{2,1,0:T(8,128)(2,1)}), bf16[8,768,256]{2,1,0:T(8,128)(2,1)}, u32[]{:S(2)}, u32[]{:S(2)}) async-start(bf16[8,768,256]{2,1,0:T(8,128)(2,1)} %bitcast.63), calls=%async_computation | async-start | bytes 6291456 | tf_op jit(solution)/shard_map/all_to_all | solution.py:47
Sparse Core Ops, SparseCore 0:
  10.0 34.3 all-gather.9
  89.2 79.9 all-reduce.1
Sparse Core Ops, SparseCore 1:
  92.1 103.4 all-gather.5
  198.0 76.1 all-gather.7
